TPU v7x, 16 devices: a whole 2x2x2 slice. The times are simulated.
16 devices in a mesh: dp: 4 (over z, y), sp: 4 (over x, core).
Axes of the slice: x: 2, y: 2, z: 2, core: 2. Of those that a mesh axis runs over, the one named last changes fastest.
Arguments:
- x_tokens: bfloat16 [64, 512, 4096], P('dp', 'sp'), parts along dimension 0
- dy_tokens: bfloat16 [64, 512, 4096], P('dp', 'sp'), parts along dimension 0
- positions: int32 [64, 512], P('dp', 'sp'), parts along dimension 0
- ln_gain: float32 [4096], replicated
- ln_bias: float32 [4096], replicated
- w_q: bfloat16 [4096, 4096], replicated
- w_k: bfloat16 [4096, 1024], replicated
- w_v: bfloat16 [4096, 1024], replicated
- w_o: bfloat16 [4096, 4096], replicated
Outputs:
- output 1: bfloat16 [64, 512, 4096], P('dp', 'sp'), parts along dimension 0
- output 2: bfloat16 [64, 512, 4096], P('dp', 'sp'), parts along dimension 0
- output 3: float32 [65536], P(('dp', 'sp')), parts along dimension 0
- output 4: float32 [65536], P(('dp', 'sp')), parts along dimension 0
There are 4 independent parts. A program takes and returns all parts, laid end to end along the dimension named above; an argument that names none is the same for every part.
All inputs are finite; a program needn't handle non-finite values.
Results may differ from a plain program's by a relative error of at most 0.0150938.
Values are sent between devices in bfloat16 or wider.
A program may use at most 1 GiB of HBM per device.

v0:
```python
import math
import jax
import jax.numpy as jnp
from jax import lax
from jax.sharding import PartitionSpec as P, NamedSharding

HEAD_DIM = 128
ROT_HALF = HEAD_DIM // 4
ROPE_BASE = 10000.0
LN_EPS = 1e-5
NEG_BIG = -1e30


def rope_tables(positions):
    inv_freq = ROPE_BASE ** (-jnp.arange(ROT_HALF, dtype=jnp.float32) / ROT_HALF)
    angles = positions.astype(jnp.float32)[:, :, None] * inv_freq
    return jnp.cos(angles)[:, :, None, :], jnp.sin(angles)[:, :, None, :]


def rotate(tensor, cos_table, sin_table):
    lower_half = tensor[..., :ROT_HALF]
    upper_half = tensor[..., ROT_HALF:2 * ROT_HALF]
    return jnp.concatenate([lower_half * cos_table - upper_half * sin_table, upper_half * cos_table + lower_half * sin_table, tensor[..., 2 * ROT_HALF:]], axis=-1)


def norm_forward(x_tokens, ln_gain, ln_bias):
    x_float = x_tokens.astype(jnp.float32)
    centered = x_float - jnp.mean(x_float, axis=-1, keepdims=True)
    inv_std = lax.rsqrt(jnp.mean(centered * centered, axis=-1, keepdims=True) + LN_EPS)
    x_hat = centered * inv_std
    normed = (x_hat * (1.0 + ln_gain) + ln_bias).astype(jnp.bfloat16)
    return normed, x_hat, inv_std


def norm_backward(d_normed, x_hat, inv_std, ln_gain):
    d_gain = jnp.sum(d_normed * x_hat, axis=(0, 1))
    d_bias = jnp.sum(d_normed, axis=(0, 1), dtype=jnp.float32)
    d_hat = d_normed * (1.0 + ln_gain)
    d_x = inv_std * (d_hat - jnp.mean(d_hat, axis=-1, keepdims=True) - x_hat * jnp.mean(d_hat * x_hat, axis=-1, keepdims=True))
    return d_x, d_gain, d_bias


def attend_forward(queries, key_heads, values, q_start, q_block):
    n_batch, q_len, kv_loc, group_size, head_dim = queries.shape
    k_len = key_heads.shape[1]
    n_blocks = q_len // q_block
    score_scale = head_dim ** -0.5
    q_blocks = queries.reshape(n_batch, n_blocks, q_block, kv_loc, group_size, head_dim)
    key_pos = jnp.arange(k_len)

    def one_block(block_idx):
        q_piece = lax.dynamic_index_in_dim(q_blocks, block_idx, axis=1, keepdims=False)
        scores = jnp.einsum('bqkgd,bskd->bkgqs', q_piece, key_heads, preferred_element_type=jnp.float32) * score_scale
        q_pos = q_start + block_idx * q_block + jnp.arange(q_block)
        scores = jnp.where(key_pos[None, :] <= q_pos[:, None], scores, NEG_BIG)
        attn_prob = jax.nn.softmax(scores, axis=-1).astype(jnp.bfloat16)
        return jnp.einsum('bkgqs,bskd->bqkgd', attn_prob, values, preferred_element_type=jnp.float32).astype(jnp.bfloat16)

    block_outs = lax.map(one_block, jnp.arange(n_blocks))
    return jnp.moveaxis(block_outs, 0, 1).reshape(n_batch, q_len, kv_loc, group_size, head_dim)


def attend_backward(queries, key_heads, values, d_attn, q_start, q_block):
    n_batch, q_len, kv_loc, group_size, head_dim = queries.shape
    k_len = key_heads.shape[1]
    n_blocks = q_len // q_block
    score_scale = head_dim ** -0.5
    q_blocks = queries.reshape(n_batch, n_blocks, q_block, kv_loc, group_size, head_dim)
    d_blocks = d_attn.reshape(n_batch, n_blocks, q_block, kv_loc, group_size, head_dim)
    key_pos = jnp.arange(k_len)

    def block_step(accums, block_idx):
        dk_acc, dv_acc = accums
        q_piece = lax.dynamic_index_in_dim(q_blocks, block_idx, axis=1, keepdims=False)
        d_piece = lax.dynamic_index_in_dim(d_blocks, block_idx, axis=1, keepdims=False)
        scores = jnp.einsum('bqkgd,bskd->bkgqs', q_piece, key_heads, preferred_element_type=jnp.float32) * score_scale
        q_pos = q_start + block_idx * q_block + jnp.arange(q_block)
        scores = jnp.where(key_pos[None, :] <= q_pos[:, None], scores, NEG_BIG)
        attn_prob = jax.nn.softmax(scores, axis=-1)
        d_prob = jnp.einsum('bqkgd,bskd->bkgqs', d_piece, values, preferred_element_type=jnp.float32)
        delta_row = jnp.sum(attn_prob * d_prob, axis=-1, keepdims=True)
        d_scores = (attn_prob * (d_prob - delta_row) * score_scale).astype(jnp.bfloat16)
        dq_piece = jnp.einsum('bkgqs,bskd->bqkgd', d_scores, key_heads, preferred_element_type=jnp.float32)
        dk_acc = dk_acc + jnp.einsum('bkgqs,bqkgd->bskd', d_scores, q_piece, preferred_element_type=jnp.float32)
        dv_acc = dv_acc + jnp.einsum('bkgqs,bqkgd->bskd', attn_prob.astype(jnp.bfloat16), d_piece, preferred_element_type=jnp.float32)
        return (dk_acc, dv_acc), dq_piece.astype(jnp.bfloat16)

    zero_acc = jnp.zeros((n_batch, k_len, kv_loc, head_dim), jnp.float32)
    (dk_acc, dv_acc), dq_blocks = lax.scan(block_step, (zero_acc, zero_acc), jnp.arange(n_blocks))
    d_query = jnp.moveaxis(dq_blocks, 0, 1).reshape(n_batch, q_len, kv_loc, group_size, head_dim)
    return d_query, dk_acc, dv_acc


def solution(mesh):
    sp_size = mesh.shape['sp']

    def local_step(x_tokens, dy_tokens, positions, ln_gain, ln_bias, w_q, w_k, w_v, w_o):
        n_batch, seq_loc, model_dim = x_tokens.shape
        n_heads = w_q.shape[1] // HEAD_DIM
        n_kv = w_k.shape[1] // HEAD_DIM
        copies = max(sp_size // n_kv, 1)
        heads_loc = n_heads // sp_size
        kv_loc = n_kv * copies // sp_size
        group_loc = heads_loc // kv_loc
        seq_len = seq_loc * sp_size
        q_block = math.gcd(seq_len, 512)
        tokens = n_batch * seq_loc

        normed, x_hat, inv_std = norm_forward(x_tokens, ln_gain, ln_bias)
        normed_flat = normed.reshape(tokens, model_dim)
        cos_table, sin_table = rope_tables(positions)
        q_lin = jnp.dot(normed_flat, w_q, preferred_element_type=jnp.float32).reshape(n_batch, seq_loc, n_heads, HEAD_DIM)
        k_lin = jnp.dot(normed_flat, w_k, preferred_element_type=jnp.float32).reshape(n_batch, seq_loc, n_kv, HEAD_DIM)
        value_rows = jnp.dot(normed_flat, w_v, preferred_element_type=jnp.float32).astype(jnp.bfloat16).reshape(n_batch, seq_loc, n_kv, HEAD_DIM)
        queries = rotate(q_lin, cos_table, sin_table).astype(jnp.bfloat16)
        key_rows = rotate(k_lin, cos_table, sin_table).astype(jnp.bfloat16)
        if copies > 1:
            key_rows = jnp.repeat(key_rows, copies, axis=2)
            value_rows = jnp.repeat(value_rows, copies, axis=2)
        q_heads = lax.all_to_all(queries, 'sp', 2, 1, tiled=True).reshape(n_batch, seq_len, kv_loc, group_loc, HEAD_DIM)
        k_heads = lax.all_to_all(key_rows, 'sp', 2, 1, tiled=True)
        v_heads = lax.all_to_all(value_rows, 'sp', 2, 1, tiled=True)
        attn_heads = attend_forward(q_heads, k_heads, v_heads, 0, q_block).reshape(n_batch, seq_len, heads_loc, HEAD_DIM)
        attn_seq = lax.all_to_all(attn_heads, 'sp', 1, 2, tiled=True).reshape(tokens, n_heads * HEAD_DIM)
        out_proj = jnp.dot(attn_seq, w_o, preferred_element_type=jnp.float32).reshape(n_batch, seq_loc, model_dim)
        out_tokens = (x_tokens.astype(jnp.float32) + out_proj).astype(jnp.bfloat16)

        d_attn = jnp.einsum('td,fd->tf', dy_tokens.reshape(tokens, model_dim), w_o, preferred_element_type=jnp.float32).astype(jnp.bfloat16).reshape(n_batch, seq_loc, n_heads, HEAD_DIM)
        d_attn_heads = lax.all_to_all(d_attn, 'sp', 2, 1, tiled=True).reshape(n_batch, seq_len, kv_loc, group_loc, HEAD_DIM)
        dq_heads, dk_heads, dv_heads = attend_backward(q_heads, k_heads, v_heads, d_attn_heads, 0, q_block)
        dq_seq = lax.all_to_all(dq_heads.reshape(n_batch, seq_len, heads_loc, HEAD_DIM), 'sp', 1, 2, tiled=True)
        if copies > 1:
            dk_seq = lax.all_to_all(dk_heads, 'sp', 1, 2, tiled=True).reshape(n_batch, seq_loc, n_kv, copies, HEAD_DIM).sum(axis=3).astype(jnp.bfloat16)
            dv_seq = lax.all_to_all(dv_heads, 'sp', 1, 2, tiled=True).reshape(n_batch, seq_loc, n_kv, copies, HEAD_DIM).sum(axis=3).astype(jnp.bfloat16)
        else:
            dk_seq = lax.all_to_all(dk_heads.astype(jnp.bfloat16), 'sp', 1, 2, tiled=True)
            dv_seq = lax.all_to_all(dv_heads.astype(jnp.bfloat16), 'sp', 1, 2, tiled=True)
        dq_lin = rotate(dq_seq, cos_table, -sin_table).astype(jnp.bfloat16).reshape(tokens, n_heads * HEAD_DIM)
        dk_lin = rotate(dk_seq, cos_table, -sin_table).astype(jnp.bfloat16).reshape(tokens, n_kv * HEAD_DIM)
        dv_lin = dv_seq.reshape(tokens, n_kv * HEAD_DIM)
        d_normed = (jnp.einsum('tf,df->td', dq_lin, w_q, preferred_element_type=jnp.float32)
                    + jnp.einsum('tf,df->td', dk_lin, w_k, preferred_element_type=jnp.float32)
                    + jnp.einsum('tf,df->td', dv_lin, w_v, preferred_element_type=jnp.float32)).astype(jnp.bfloat16).reshape(n_batch, seq_loc, model_dim)
        d_x, d_gain, d_bias = norm_backward(d_normed, x_hat, inv_std, ln_gain)
        dx_tokens = (dy_tokens.astype(jnp.float32) + d_x).astype(jnp.bfloat16)
        return out_tokens, dx_tokens, d_gain, d_bias

    tok_spec = P('dp', 'sp', None)
    rep_vec = P(None)
    rep_mat = P(None, None)
    part_vec = P(('dp', 'sp'))
    return jax.shard_map(local_step, mesh=mesh,
                         in_specs=(tok_spec, tok_spec, P('dp', 'sp'), rep_vec, rep_vec, rep_mat, rep_mat, rep_mat, rep_mat),
                         out_specs=(tok_spec, tok_spec, part_vec, part_vec), check_vma=False)
```

profile of v0, /device:TPU:0, one launch (start us, length us, event | category | flops | bytes accessed | tf_op | source)
XLA Modules:
  0.0 1962.6 jit_solution(3371292939605097221)
XLA Ops:
  1.5 8.7 convert_reduce_fusion
  16.9 11.9 copy.92
  28.8 12.3 fusion.19
  41.2 19.8 %fusion.39 = f32[16,128,8,128]{1,3,2,0:T(8,128)} fusion(bf16[8,128,4096,1]{2,1,0,3:T(8,128)(2,1)S(1)} %bitcast.205, bf16[16,128,4096]{2,1,0:T(8,128)(2,1)S(1)} %fusion.19), kind=kOutput, calls=%fused_computation.52 | convolution fusion | flops 17179869184 | bytes 33554432 | tf_op jit(solution)/shard_map/dot_general | solution.py:113
  71.6 17.0 all-to-all-start.1
  88.6 22.7 %convert_bitcast_fusion.1 = bf16[256,8,8,128]{3,1,2,0:T(8,128)(2,1)S(1)} fusion(bf16[2048,4096]{1,0:T(8,128)(2,1)} %bitcast.194, bf16[4096,1024]{1,0:T(8,128)(2,1)} %param.16), kind=kOutput, calls=%fused_computation.83 | convolution fusion | flops 17181966336 | bytes 29360128 | tf_op jit(solution)/shard_map/dot_general | solution.py:114
  115.6 21.9 %all-to-all-done.1 = bf16[16,128,8,128]{1,3,0,2:T(8,128)(2,1)} async-done(((bf16[16,128,8,128]{1,3,0,2:T(8,128)(2,1)}), bf16[16,128,8,128]{1,3,0,2:T(8,128)(2,1)}, u32[]{:S(2)}, u32[]{:S(2)}) %all-to-all-start.1) | async-done | bytes 4194336 | tf_op jit(solution)/shard_map/all_to_all | solution.py:121
  142.3 79.9 %convert_bitcast_fusion = bf16[256,8,32,128]{3,1,2,0:T(8,128)(2,1)} fusion(bf16[2048,4096]{1,0:T(8,128)(2,1)} %bitcast.203, bf16[4096,4096]{1,0:T(8,128)(2,1)} %param.17), kind=kOutput, calls=%fused_computation.56 | convolution fusion | flops 68727865344 | bytes 67108864 | tf_op jit(solution)/shard_map/td,fd->tf/dot_general | solution.py:128
  222.2 9.6 copy.99
  231.9 18.7 copy.61
  250.6 41.0 %copy.93 = bf16[4096,4096]{1,0:T(8,128)(2,1)} copy(bf16[4096,4096]{0,1:T(8,128)(2,1)} %bitcast.191) | data formatting | bytes 67108864 | tf_op jit(solution)/shard_map/dot_general | solution.py:112
  291.6 7.4 all-to-all-start.4
  299.1 78.7 %fusion.37 = f32[16,128,32,128]{1,3,2,0:T(8,128)} fusion(bf16[32,128,4096,1]{2,1,0,3:T(8,128)(2,1)} %bitcast.192, bf16[16,128,4096]{2,1,0:T(8,128)(2,1)} %copy-done.2), kind=kOutput, calls=%fused_computation.50 | convolution fusion | flops 68719476736 | bytes 83886080 | tf_op jit(solution)/shard_map/dot_general | solution.py:112
  384.9 7.3 subtract_convert_fusion
  401.1 80.6 %all-to-all-done.4 = bf16[16,128,32,128]{3,1,0,2:T(8,128)(2,1)} async-done(((bf16[16,128,32,128]{3,1,0,2:T(8,128)(2,1)}), bf16[16,128,32,128]{3,1,0,2:T(8,128)(2,1)}, u32[]{:S(2)}, u32[]{:S(2)}) %all-to-all-start.4) | async-done | bytes 16777248 | tf_op jit(solution)/shard_map/all_to_all | solution.py:129
  495.5 7.5 copy.51
  502.9 7.3 copy.96
  510.2 14.2 copy.62
  524.4 147.3 %all-to-all-done.2 = bf16[16,128,32,128]{1,3,0,2:T(8,128)(2,1)} async-done(((bf16[16,128,32,128]{1,3,0,2:T(8,128)(2,1)}), bf16[16,128,32,128]{1,3,0,2:T(8,128)(2,1)}, u32[]{:S(2)}, u32[]{:S(2)}) %all-to-all-start.2) | async-done | bytes 16777248 | tf_op jit(solution)/shard_map/all_to_all | solution.py:120
  671.6 21.6 %copy.57 = bf16[16,128,4,8,128]{4,1,2,3,0:T(8,128)(2,1)} copy(bf16[16,128,4,8,128]{1,4,0,3,2:T(8,128)(2,1)} %bitcast.18) | data formatting | bytes 33554432 | tf_op jit(solution)/shard_map/all_to_all | solution.py:120
  693.2 50.7 %fusion.75 = f32[16,2,512,512,4]{3,2,4,1,0:T(8,128)} fusion(bf16[16,512,2,128,1]{3,1,4,2,0:T(8,128)(2,1)} %bitcast.193, bf16[16,512,2,4,128]{4,1,3,2,0:T(8,128)(2,1)} %bitcast.183), kind=kOutput, calls=%fused_computation.111 | convolution fusion | flops 8589934592 | bytes 155189248 | tf_op jit(solution)/shard_map/while/body/eval_jaxpr/bqkgd,bskd->bkgqs/dot_general | solution.py:80
  744.0 58.6 %fusion.74 = (f32[16,2,4,512]{3,2,1,0:T(4,128)S(1)}, f32[16,2,4,512,512]{3,4,2,1,0:T(8,128)}) fusion(pred[512,512]{0,1:T(8,128)(4,1)S(1)} %iota_compare_fusion, bf16[16,512,2,128,1]{3,1,4,2,0:T(8,128)(2,1)} %bitcast.207, bf16[16,512,2,4,128]{4,1,3,2,0:T(8,128)(2,1)} %bitcast.195), kind=kOutput, calls=%fused_computation.110 | convolution fusion | flops 8724152320 | bytes 155713536 | tf_op jit(solution)/shard_map/while/body/eval_jaxpr/sub | solution.py:56
  802.5 168.8 %fusion.53 = bf16[16,512,2,128]{1,3,2,0:T(8,128)(2,1)} fusion(bf16[16,512,2,4,128]{4,1,3,2,0:T(8,128)(2,1)} %bitcast.196, f32[16,2,512,512,4]{3,2,4,1,0:T(8,128)} %fusion.75, f32[16,2,4,512,512]{3,4,2,1,0:T(8,128)} %get-tuple-element.65, f32[16,2,4,512]{3,2,1,0:T(4,128)S(1)} %get-tuple-element.64), kind=kOutput, calls=%fused_computation.72 | convolution fusion | flops 8826978304 | bytes 289669120 | tf_op jit(solution)/shard_map/while/body/eval_jaxpr/bkgqs,bqkgd->bskd/dot_general | solution.py:84
  971.4 11.3 copy.72
  987.8 49.4 %fusion.54 = bf16[16,512,2,128]{1,3,2,0:T(8,128)(2,1)} fusion(bf16[16,512,2,4,128]{4,1,3,2,0:T(8,128)(2,1)} %bitcast.184, f32[16,2,4,512,512]{3,4,2,1,0:T(8,128)} %get-tuple-element.65, f32[16,2,4,512]{3,2,1,0:T(4,128)S(1)} %get-tuple-element.64), kind=kOutput, calls=%fused_computation.73 | convolution fusion | flops 8659140608 | bytes 155451392 | tf_op jit(solution)/shard_map/while/body/eval_jaxpr/bkgqs,bqkgd->bskd/dot_general | solution.py:85
  1037.2 11.1 copy.77
  1053.3 165.7 %fusion.43 = bf16[16,2,128,4,512]{4,2,3,1,0:T(8,128)(2,1)} fusion(bf16[16,512,2,128,1]{3,1,4,2,0:T(8,128)(2,1)} %bitcast.208, f32[16,2,512,512,4]{3,2,4,1,0:T(8,128)} %fusion.75, f32[16,2,4,512,512]{3,4,2,1,0:T(8,128)} %get-tuple-element.65, f32[16,2,4,512]{3,2,1,0:T(4,128)S(1)} %get-tuple-element.64), kind=kOutput, calls=%fused_computation.62 | convolution fusion | flops 8833269760 | bytes 289669120 | tf_op jit(solution)/shard_map/while/body/eval_jaxpr/bkgqs,bskd->bqkgd/dot_general | solution.py:83
  1219.0 23.6 %copy.66 = bf16[16,512,8,128]{3,2,0,1:T(8,128)(2,1)} copy(bf16[16,512,8,128]{1,3,2,0:T(8,128)(2,1)} %bitcast.198) | data formatting | bytes 33554432 | tf_op jit(solution)/shard_map/reshape;reshape;transpose | solution.py:131
  1249.6 7.2 reshape.106
  1256.8 48.9 %fusion.44 = bf16[16,2,128,4,512]{4,2,3,1,0:T(8,128)(2,1)} fusion(bf16[16,512,2,128,1]{1,3,2,0,4:T(8,128)(2,1)} %reshape.106, f32[16,2,4,512,512]{3,4,2,1,0:T(8,128)} %get-tuple-element.65, f32[16,2,4,512]{3,2,1,0:T(4,128)S(1)} %get-tuple-element.64), kind=kOutput, calls=%fused_computation.63 | convolution fusion | flops 8665432064 | bytes 155451392 | tf_op jit(solution)/shard_map/while/body/eval_jaxpr/bkgqs,bskd->bqkgd/dot_general | solution.py:57
  1305.7 23.5 %copy.59 = bf16[16,512,8,128]{3,2,0,1:T(8,128)(2,1)} copy(bf16[16,512,8,128]{1,3,2,0:T(8,128)(2,1)} %bitcast.197) | data formatting | bytes 33554432 | tf_op jit(solution)/shard_map/reshape;reshape;transpose | solution.py:123
  1329.2 103.1 %all-to-all-done.5 = bf16[16,512,8,128]{3,2,0,1:T(8,128)(2,1)} async-done(((bf16[16,512,8,128]{3,2,0,1:T(8,128)(2,1)}), bf16[16,512,8,128]{3,2,0,1:T(8,128)(2,1)}, u32[]{:S(2)}, u32[]{:S(2)}) %all-to-all-start.5) | async-done | bytes 16777248 | tf_op jit(solution)/shard_map/all_to_all | solution.py:131
  1432.3 7.5 all-to-all-start.3
  1439.8 11.0 copy.73
  1450.9 8.4 copy.78
  1472.4 25.2 %fusion.57 = f32[2048,4096]{1,0:T(8,128)} fusion(bf16[4096,1024]{1,0:T(8,128)(2,1)} %param.15, bf16[256,8,8,128]{3,2,1,0:T(8,128)(2,1)} %bitcast.209), kind=kOutput, calls=%fused_computation.76 | convolution fusion | flops 17179869184 | bytes 46137344 | tf_op jit(solution)/shard_map/tf,df->td/dot_general | solution.py:142
  1497.5 25.1 %copy.68 = bf16[16,128,4,8,128]{1,4,3,2,0:T(8,128)(2,1)} copy(bf16[16,128,4,8,128]{4,3,0,1,2:T(8,128)(2,1)} %bitcast.40) | data formatting | bytes 33554432 | tf_op jit(solution)/shard_map/all_to_all | solution.py:131
  1522.6 9.4 slice.58
  1539.1 83.4 %all-to-all-done.3 = bf16[16,512,8,128]{3,2,0,1:T(8,128)(2,1)} async-done(((bf16[16,512,8,128]{3,2,0,1:T(8,128)(2,1)}), bf16[16,512,8,128]{3,2,0,1:T(8,128)(2,1)}, u32[]{:S(2)}, u32[]{:S(2)}) %all-to-all-start.3) | async-done | bytes 16777248 | tf_op jit(solution)/shard_map/all_to_all | solution.py:124
  1622.5 14.7 copy.118
  1637.2 25.3 %dot_general.69 = bf16[16,128,4096]{2,1,0:T(8,128)(2,1)} reshape(bf16[16,128,4,8,128]{4,3,2,1,0:T(8,128)(2,1)} %bitcast.188) | data formatting | bytes 33554432 | tf_op jit(solution)/shard_map/dot_general | solution.py:125
  1662.5 80.6 %fusion.27 = bf16[16,128,4096]{2,1,0:T(8,128)(2,1)} fusion(bf16[16,128,4096]{2,1,0:T(8,128)(2,1)} %param.9, bf16[16,128,4096]{2,1,0:T(8,128)(2,1)} %dot_general.69, bf16[4096,4096]{1,0:T(8,128)(2,1)} %param.17), kind=kOutput, calls=%fused_computation.35 | convolution fusion | flops 68744642560 | bytes 83886080 | tf_op jit(solution)/shard_map/dot_general | solution.py:125
  1743.1 9.2 pad_maximum_fusion.1
  1752.3 23.2 %copy.69 = bf16[16,128,32,128]{3,2,1,0:T(8,128)(2,1)} copy(bf16[16,128,32,128]{1,3,2,0:T(8,128)(2,1)} %pad_maximum_fusion.1) | data formatting | bytes 33554432 | tf_op jit(solution)/shard_map/concatenate | solution.py:23
  1775.5 92.8 %fusion.34 = f32[2048,4096]{1,0:T(8,128)} fusion(bf16[4096,4096]{1,0:T(8,128)(2,1)} %param.14, bf16[256,8,32,128]{3,2,1,0:T(8,128)(2,1)} %bitcast.199), kind=kOutput, calls=%fused_computation.44 | convolution fusion | flops 68719476736 | bytes 83886080 | tf_op jit(solution)/shard_map/tf,df->td/dot_general | solution.py:141
  1868.3 40.3 %convert_reduce_fusion.1 = (f32[4096]{0:T(1024)}, f32[2048]{0:T(1024)S(1)}, bf16[2048,4096]{1,0:T(8,128)(2,1)}) fusion(f32[4096]{0:T(1024)S(1)} %copy-done.12, bf16[4096,1024]{1,0:T(8,128)(2,1)} %param.16, bf16[128,8,16,128]{3,2,1,0:T(8,128)(2,1)} %bitcast.206, f32[2048,4096]{1,0:T(8,128)} %fusion.34, f32[2048,4096]{1,0:T(8,128)} %fusion.57), kind=kOutput, calls=%fused_computation.55 | convolution fusion | flops 17238583296 | bytes 96509952 | tf_op jit(solution)/shard_map/tf,df->td/dot_general | solution.py:143
  1908.6 25.3 %fusion.25 = (f32[4096]{0:T(1024)}, f32[16,128]{1,0:T(8,128)S(1)}) fusion(bf16[16,128,4096]{2,1,0:T(8,128)(2,1)} %param.9, f32[16,128]{1,0:T(8,128)S(1)} %copy-done.16, f32[16,128]{1,0:T(8,128)S(1)} %copy-done.14, bf16[2048,4096]{1,0:T(8,128)(2,1)} %get-tuple-element.66, f32[4096]{0:T(1024)S(1)} %copy-done.12, bf16[16,128,4096]{2,1,0:T(8,128)(2,1)} %bitcast.182), kind=kLoop, calls=%fused_computation.33 | loop fusion | flops 83879936 | bytes 50388992 | tf_op jit(solution)/shard_map/reduce_sum | solution.py:36
  1934.0 28.2 %fusion.24 = bf16[16,128,4096]{2,1,0:T(8,128)(2,1)} fusion(bf16[16,128,4096]{2,1,0:T(8,128)(2,1)} %param.9, bf16[16,128,4096]{2,1,0:T(8,128)(2,1)} %param.10, f32[16,128]{1,0:T(8,128)S(1)} %broadcast_multiply_fusion, f32[16,128]{1,0:T(8,128)S(1)} %multiply_bitcast_fusion, f32[4096]{0:T(1024)S(1)} %copy-done.12, f32[16,128]{1,0:T(8,128)S(1)} %copy-done.16, ...), kind=kLoop, calls=%fused_computation.32 | loop fusion | flops 100663296 | bytes 67158016 | tf_op jit(solution)/shard_map/convert_element_type | solution.py:145
  (71 shorter events, 94.0 us)
Async XLA Ops:
  0.6 10.7 copy-start
  1.5 15.4 copy-start.18
  11.3 17.5 copy-start.13
  11.3 17.5 copy-start.17
  16.9 24.3 %copy-start.15 = (f32[16,128]{1,0:T(8,128)}, f32[16,128]{1,0:T(8,128)S(1)}, u32[]{:S(2)}) copy-start(f32[16,128]{1,0:T(8,128)S(1)} %add_rsqrt_fusion) | copy-start | bytes 24580
  16.9 24.3 %copy-start.11 = (f32[4096]{0:T(1024)}, f32[4096]{0:T(1024)S(1)}, u32[]{:S(2)}) copy-start(f32[4096]{0:T(1024)S(1)} %broadcast_add_fusion) | copy-start | bytes 49156
  28.8 12.4 copy-start.4
  41.2 19.8 %copy-start.2 = (bf16[16,128,4096]{2,1,0:T(8,128)(2,1)}, bf16[16,128,4096]{2,1,0:T(8,128)(2,1)S(1)}, u32[]{:S(2)}) copy-start(bf16[16,128,4096]{2,1,0:T(8,128)(2,1)S(1)} %fusion.19) | copy-start | bytes 50331652
  65.5 3.2 copy-start.5
  65.5 3.2 copy-start.9
  71.6 65.9 %all-to-all-start.1 = ((bf16[16,128,8,128]{1,3,0,2:T(8,128)(2,1)}), bf16[16,128,8,128]{1,3,0,2:T(8,128)(2,1)}, u32[]{:S(2)}, u32[]{:S(2)}) async-start(bf16[16,128,8,128]{1,3,0,2:T(8,128)(2,1)} %copy.53), calls=%async_computation.1 | async-start | bytes 8388608 | tf_op jit(solution)/shard_map/all_to_all | solution.py:121
  137.5 154.2 %all-to-all-start = ((bf16[16,128,8,128]{3,1,0,2:T(8,128)(2,1)}), bf16[16,128,8,128]{3,1,0,2:T(8,128)(2,1)}, u32[]{:S(2)}, u32[]{:S(2)}) async-start(bf16[16,128,8,128]{3,1,0,2:T(8,128)(2,1)} %copy.50), calls=%async_computation | async-start | bytes 8388608 | tf_op jit(solution)/shard_map/all_to_all | solution.py:122
  291.6 190.1 %all-to-all-start.4 = ((bf16[16,128,32,128]{3,1,0,2:T(8,128)(2,1)}), bf16[16,128,32,128]{3,1,0,2:T(8,128)(2,1)}, u32[]{:S(2)}, u32[]{:S(2)}) async-start(bf16[16,128,32,128]{3,1,0,2:T(8,128)(2,1)} %copy.61), calls=%async_computation.4 | async-start | bytes 33554432 | tf_op jit(solution)/shard_map/all_to_all | solution.py:129
  377.8 7.0 copy-start.6
  377.8 7.0 copy-start.10
  481.8 189.9 %all-to-all-start.2 = ((bf16[16,128,32,128]{1,3,0,2:T(8,128)(2,1)}), bf16[16,128,32,128]{1,3,0,2:T(8,128)(2,1)}, u32[]{:S(2)}, u32[]{:S(2)}) async-start(bf16[16,128,32,128]{1,3,0,2:T(8,128)(2,1)} %copy.56), calls=%async_computation.2 | async-start | bytes 33554432 | tf_op jit(solution)/shard_map/all_to_all | solution.py:120
  982.6 65.7 %all-to-all-start.6 = ((bf16[16,512,2,128]{3,2,0,1:T(2,128)(2,1)}), bf16[16,512,2,128]{3,2,0,1:T(2,128)(2,1)}, u32[]{:S(2)}, u32[]{:S(2)}) async-start(bf16[16,512,2,128]{3,2,0,1:T(2,128)(2,1)} %copy.72), calls=%async_computation.6 | async-start | bytes 8388608 | tf_op jit(solution)/shard_map/all_to_all | solution.py:136
  1048.3 194.3 %all-to-all-start.7 = ((bf16[16,512,2,128]{3,2,0,1:T(2,128)(2,1)}), bf16[16,512,2,128]{3,2,0,1:T(2,128)(2,1)}, u32[]{:S(2)}, u32[]{:S(2)}) async-start(bf16[16,512,2,128]{3,2,0,1:T(2,128)(2,1)} %copy.77), calls=%async_computation.7 | async-start | bytes 8388608 | tf_op jit(solution)/shard_map/all_to_all | solution.py:137
  1242.6 189.7 %all-to-all-start.5 = ((bf16[16,512,8,128]{3,2,0,1:T(8,128)(2,1)}), bf16[16,512,8,128]{3,2,0,1:T(8,128)(2,1)}, u32[]{:S(2)}, u32[]{:S(2)}) async-start(bf16[16,512,8,128]{3,2,0,1:T(8,128)(2,1)} %copy.66), calls=%async_computation.5 | async-start | bytes 33554432 | tf_op jit(solution)/shard_map/all_to_all | solution.py:131
  1432.3 190.2 %all-to-all-start.3 = ((bf16[16,512,8,128]{3,2,0,1:T(8,128)(2,1)}), bf16[16,512,8,128]{3,2,0,1:T(8,128)(2,1)}, u32[]{:S(2)}, u32[]{:S(2)}) async-start(bf16[16,512,8,128]{3,2,0,1:T(8,128)(2,1)} %copy.59), calls=%async_computation.3 | async-start | bytes 33554432 | tf_op jit(solution)/shard_map/all_to_all | solution.py:124
  1439.8 21.3 %copy-start.7 = (f32[16,128,32]{1,2,0:T(8,128)S(1)}, f32[16,128,32]{1,2,0:T(8,128)}, u32[]{:S(2)}) copy-start(f32[16,128,32]{1,2,0:T(8,128)} %copy-done.5) | copy-start | bytes 786436
  1439.8 21.3 %copy-start.8 = (f32[16,128,32]{1,2,0:T(8,128)S(1)}, f32[16,128,32]{1,2,0:T(8,128)}, u32[]{:S(2)}) copy-start(f32[16,128,32]{1,2,0:T(8,128)} %get-tuple-element.61) | copy-start | bytes 786436
  1662.5 80.6 %copy-start.1 = (bf16[16,128,32,64]{1,3,2,0:T(8,128)(2,1)S(1)}, bf16[16,128,32,64]{1,3,2,0:T(8,128)(2,1)}, u32[]{:S(2)}) copy-start(bf16[16,128,32,64]{1,3,2,0:T(8,128)(2,1)} %slice.58) | copy-start | bytes 25165828
  1662.5 80.6 %copy-start.3 = (bf16[16,128,32,32]{1,3,2,0:T(8,128)(2,1)S(1)}, bf16[16,128,32,32]{1,3,2,0:T(8,128)(2,1)}, u32[]{:S(2)}) copy-start(bf16[16,128,32,32]{1,3,2,0:T(8,128)(2,1)} %get-tuple-element.46) | copy-start | bytes 12582916
  1775.5 92.8 %copy-start.12 = (f32[4096]{0:T(1024)S(1)}, f32[4096]{0:T(1024)}, u32[]{:S(2)}) copy-start(f32[4096]{0:T(1024)} %copy-done.11) | copy-start | bytes 49156
  1868.3 40.3 %copy-start.14 = (f32[16,128]{1,0:T(8,128)S(1)}, f32[16,128]{1,0:T(8,128)}, u32[]{:S(2)}) copy-start(f32[16,128]{1,0:T(8,128)} %copy-done.13) | copy-start | bytes 24580
  1868.3 40.3 %copy-start.16 = (f32[16,128]{1,0:T(8,128)S(1)}, f32[16,128]{1,0:T(8,128)}, u32[]{:S(2)}) copy-start(f32[16,128]{1,0:T(8,128)} %copy-done.15) | copy-start | bytes 24580
where the time goes:
time: 1970 us; the launch traced here: 1960 us
  matrix products  982 us (50%)
  waiting for transfers between devices  436 us (22%)
  local copies, waits for them, and re-layouts  365 us (19%)
  other arithmetic  117 us (6%)
  starting transfers between devices  61 us (3%)
    dot_general x1, matrix products, block_step(): jnp.einsum('bkgqs,bqkgd->bskd', d_scores, q_piece, preferred_element_type...  169 us
    dot_general x1, matrix products, block_step(): jnp.einsum('bkgqs,bskd->bqkgd', d_scores, key_heads, preferred_element_ty...  166 us
    all_to_all x1, waiting for transfers between devices, local_step(): lax.all_to_all(queries, 'sp', 2, 1, tiled=True)  147 us
    all_to_all x1, waiting for transfers between devices, local_step(): lax.all_to_all(dq_heads.reshape(n_batch, seq_len, heads_loc, HEAD_DIM), '...  103 us
    dot_general x1, matrix products, local_step(): jnp.einsum('tf,df->td', dq_lin, w_q, preferred_element_type=jnp.float32)  92.8 us
    all_to_all x1, waiting for transfers between devices, local_step(): lax.all_to_all(attn_heads, 'sp', 1, 2, tiled=True)  83.4 us
    all_to_all x1, waiting for transfers between devices, local_step(): lax.all_to_all(d_attn, 'sp', 2, 1, tiled=True)  80.6 us
    dot_general x1, matrix products, local_step(): jnp.dot(attn_seq, w_o, preferred_element_type=jnp.float32)  80.6 us
  transfers between devices with their start and end apart: 8, of which 5 were waited for; matrix products, arithmetic and copies ran while one was open for 38% of the time, Pallas kernels for 0%

commit v1 on v0

v1 whole, which is shorter than its diff:
```python
import math
import jax
import jax.numpy as jnp
from jax import lax
from jax.experimental import pallas as pl
from jax.experimental.pallas import tpu as pltpu
from jax.sharding import PartitionSpec as P

HEAD_DIM = 128
ROT_HALF = HEAD_DIM // 4
ROPE_BASE = 10000.0
LN_EPS = 1e-5
NEG_BIG = -1e30
CHUNKS = 4
HALVES = 2
SCALE = HEAD_DIM ** -0.5
EXP_SCALE = SCALE * math.log2(math.e)
KV_WIDTH = 2 * HEAD_DIM


PAIRS_A = [(0, 1), (2, 3)]
PAIRS_B = [(0, 2), (1, 3)]
PAIRS_C = [(2, 3), (3, 2)]


def reverse(pairs):
    return [(target, source) for source, target in pairs]


def rope_tables(positions):
    inv_freq = ROPE_BASE ** (-jnp.arange(ROT_HALF, dtype=jnp.float32) / ROT_HALF)
    angles = positions.astype(jnp.float32)[:, None] * inv_freq
    cos, sin = jnp.cos(angles), jnp.sin(angles)
    zero = jnp.zeros_like(sin)
    one = jnp.ones_like(sin)
    return jnp.concatenate([cos, cos, one, one, -sin, zero, zero, zero, zero, sin, zero, zero], axis=1)


def rotate(tensor, table, sign):
    cos = table[:, :HEAD_DIM]
    sin_low = table[:, HEAD_DIM:2 * HEAD_DIM]
    sin_high = table[:, 2 * HEAD_DIM:]
    turned = pltpu.roll(tensor, HEAD_DIM - ROT_HALF, 1) * sin_low + pltpu.roll(tensor, ROT_HALF, 1) * sin_high
    return tensor * cos + turned if sign > 0 else tensor * cos - turned


def pack_kernel(table_ref, lin_ref, *rest):
    out_ref = rest[-1]
    table = table_ref[...]
    for head in range(lin_ref.shape[1] // KV_WIDTH):
        k_cols = slice(head * KV_WIDTH, head * KV_WIDTH + HEAD_DIM)
        v_cols = slice(head * KV_WIDTH + HEAD_DIM, (head + 1) * KV_WIDTH)
        out_ref[:, k_cols] = rotate(lin_ref[:, k_cols], table, 1).astype(jnp.bfloat16)
        out_ref[:, v_cols] = lin_ref[:, v_cols].astype(jnp.bfloat16)


def join_kernel(wk_ref, wv_ref, out_ref):
    for head in range(wk_ref.shape[1] // HEAD_DIM):
        cols = slice(head * HEAD_DIM, (head + 1) * HEAD_DIM)
        out_ref[:, head * KV_WIDTH:head * KV_WIDTH + HEAD_DIM] = wk_ref[:, cols]
        out_ref[:, head * KV_WIDTH + HEAD_DIM:(head + 1) * KV_WIDTH] = wv_ref[:, cols]


def add_kernel(left_ref, right_ref, out_ref):
    out_ref[...] = left_ref[...] + right_ref[...]


def finish_kernel(table_ref, own_ref, a_ref, b_ref, *rest):
    out_ref = rest[-1]
    table = table_ref[...]
    for head in range(own_ref.shape[1] // KV_WIDTH):
        k_cols = slice(head * KV_WIDTH, head * KV_WIDTH + HEAD_DIM)
        v_cols = slice(head * KV_WIDTH + HEAD_DIM, (head + 1) * KV_WIDTH)
        d_key = (own_ref[:, k_cols] + a_ref[:, k_cols] + b_ref[:, k_cols]).astype(jnp.bfloat16).astype(jnp.float32)
        d_val = own_ref[:, v_cols] + a_ref[:, v_cols] + b_ref[:, v_cols]
        out_ref[:, k_cols] = rotate(d_key, table, -1).astype(jnp.bfloat16)
        out_ref[:, v_cols] = d_val.astype(jnp.bfloat16)


def dot(lhs, rhs, contract):
    return lax.dot_general(lhs, rhs, (contract, ((), ())), preferred_element_type=jnp.float32)


def attend_kernel(flags_ref, table_ref, q_ref, do_ref, own_ref, a_ref, b_ref, c_ref, *rest):
    o_ref, dq_ref, d_own_ref, d_a_ref, d_b_ref, d_c_ref = rest[-6:]
    seq = q_ref.shape[0]
    table = table_ref[...]
    kv_refs = (own_ref, a_ref, b_ref, c_ref)
    d_refs = (d_own_ref, d_a_ref, d_b_ref, d_c_ref)
    keys = jnp.concatenate([ref[:, :HEAD_DIM] for ref in kv_refs], axis=0)
    values = jnp.concatenate([ref[:, HEAD_DIM:] for ref in kv_refs], axis=0)
    keys_t = keys.T
    values_t = values.T
    off_a = (1 - flags_ref[0]).astype(jnp.float32) * 1e30
    off_bc = (1 - flags_ref[1]).astype(jnp.float32) * 1e30
    offsets = (None, off_a, off_bc, off_bc)
    n_heads = q_ref.shape[1] // HEAD_DIM
    step = 2
    d_keys = None
    d_values = None
    key_pos = lax.broadcasted_iota(jnp.int32, (seq, step * seq), 0)
    query_pos = lax.broadcasted_iota(jnp.int32, (seq, step * seq), 1) % seq
    visible = key_pos <= query_pos
    for first in range(0, n_heads, step):
        cols = [slice(h * HEAD_DIM, (h + 1) * HEAD_DIM) for h in range(first, first + step)]
        q = jnp.concatenate([rotate(q_ref[:, col], table, 1).astype(jnp.bfloat16) for col in cols], axis=0)
        d_out = jnp.concatenate([do_ref[:, col] for col in cols], axis=0)
        scores = dot(keys, q, ((1,), (1,)))
        parts = [scores[j * seq:(j + 1) * seq] for j in range(4)]
        parts[0] = jnp.where(visible, parts[0], NEG_BIG)
        peak = jnp.max(parts[0], axis=0, keepdims=True)
        for part, off in zip(parts[1:], offsets[1:]):
            peak = jnp.maximum(peak, jnp.max(part, axis=0, keepdims=True) - off)
        peak = peak * EXP_SCALE
        weights = [jnp.exp2(parts[0] * EXP_SCALE - peak)]
        for part, off in zip(parts[1:], offsets[1:]):
            weights.append(jnp.exp2(part * EXP_SCALE - (peak + off)))
        total = sum(jnp.sum(w, axis=0, keepdims=True) for w in weights)
        prob = jnp.concatenate(weights, axis=0) * (1.0 / total)
        prob_b = prob.astype(jnp.bfloat16)
        d_prob = dot(values, d_out, ((1,), (1,)))
        delta = jnp.sum(prob * d_prob, axis=0, keepdims=True)
        d_scores = (prob * (d_prob - delta)).astype(jnp.bfloat16)
        out_t = dot(values_t, prob_b, ((1,), (0,))).astype(jnp.bfloat16)
        dq_t = dot(keys_t, d_scores, ((1,), (0,))) * SCALE
        for i, col in enumerate(cols):
            lanes = slice(i * seq, (i + 1) * seq)
            o_ref[:, col] = out_t[:, lanes].T
            dq = dq_t[:, lanes].T.astype(jnp.bfloat16).astype(jnp.float32)
            dq_ref[:, col] = rotate(dq, table, -1).astype(jnp.bfloat16)
        d_k = dot(d_scores, q, ((1,), (0,)))
        d_v = dot(prob_b, d_out, ((1,), (0,)))
        d_keys = d_k if d_keys is None else d_keys + d_k
        d_values = d_v if d_values is None else d_values + d_v
    d_keys = d_keys * SCALE
    for j, ref in enumerate(d_refs):
        ref[:, :HEAD_DIM] = d_keys[j * seq:(j + 1) * seq]
        ref[:, HEAD_DIM:] = d_values[j * seq:(j + 1) * seq]


def solution(mesh):
    def block_step(x_tokens, dy_tokens, positions, ln_gain, ln_bias, w_q, w_k, w_v, w_o):
        n_batch, seq, model_dim = x_tokens.shape
        n_kv = w_k.shape[1] // HEAD_DIM
        group = w_q.shape[1] // w_k.shape[1]
        q_width = group * HEAD_DIM
        kv_cols = n_kv * KV_WIDTH
        tokens = n_batch * seq
        rows_b = n_batch // CHUNKS
        chunk_rows = rows_b * seq
        x_flat = x_tokens.reshape(tokens, model_dim)
        dy_flat = dy_tokens.reshape(tokens, model_dim)
        rank = lax.axis_index('sp')
        flags = jnp.stack([rank % 2, rank // 2]).astype(jnp.int32)

        x_float = x_flat.astype(jnp.float32)
        centered = x_float - jnp.mean(x_float, axis=-1, keepdims=True)
        inv_std = lax.rsqrt(jnp.mean(centered * centered, axis=-1, keepdims=True) + LN_EPS)
        x_hat = centered * inv_std
        normed = (x_hat * (1.0 + ln_gain) + ln_bias).astype(jnp.bfloat16)
        table = rope_tables(positions.reshape(tokens))
        w_rows = math.gcd(model_dim, 512)
        w_kv = pl.pallas_call(
            join_kernel, grid=(model_dim // w_rows,), in_specs=[pl.BlockSpec((w_rows, kv_cols // 2), lambda i: (i, 0))] * 2,
            out_specs=pl.BlockSpec((w_rows, kv_cols), lambda i: (i, 0)), out_shape=jax.ShapeDtypeStruct((model_dim, kv_cols), jnp.bfloat16), name='join_kv',
            cost_estimate=pl.CostEstimate(flops=model_dim * kv_cols * 300, bytes_accessed=model_dim * kv_cols * 4, transcendentals=0),
        )(w_k, w_v)
        kv_lin = jnp.dot(normed, w_kv, preferred_element_type=jnp.float32)

        table_width = 3 * HEAD_DIM

        def row_spec(width, base=0):
            return pl.BlockSpec((seq, width), lambda b: (b + base, 0))

        def pack(chunk, before):
            base = chunk * rows_b
            return pl.pallas_call(
                pack_kernel, grid=(rows_b,),
                in_specs=[row_spec(table_width, base), row_spec(kv_cols, base)] + [pl.BlockSpec(memory_space=pl.ANY)] * len(before), out_specs=row_spec(kv_cols),
                out_shape=jax.ShapeDtypeStruct((chunk_rows, kv_cols), jnp.bfloat16), name='pack_kv',
                cost_estimate=pl.CostEstimate(flops=chunk_rows * kv_cols * 300, bytes_accessed=chunk_rows * kv_cols * 6, transcendentals=0),
            )(table, kv_lin, *before)

        def send(value, pairs):
            return lax.ppermute(value, 'sp', pairs)

        own = []
        for c in range(CHUNKS):
            own.append(pack(c, own[-1:]))
        from_b = [send(own[c], PAIRS_B) for c in range(CHUNKS)]
        from_a = [send(own[c], PAIRS_A) for c in range(CHUNKS)]
        from_c = [send(from_b[c], PAIRS_C) for c in range(CHUNKS)]

        half_rows = tokens // HALVES
        q_half, da_half = [], []
        for i in range(HALVES):
            rows = slice(i * half_rows, (i + 1) * half_rows)
            q_half.append(jnp.dot(normed[rows], w_q, preferred_element_type=jnp.float32))
            da_half.append(jnp.einsum('td,fd->tf', dy_flat[rows], w_o, preferred_element_type=jnp.float32).astype(jnp.bfloat16))

        def attend(chunk, carried):
            base = chunk * rows_b
            half = chunk * HALVES // CHUNKS
            half_base = base - half * (n_batch // HALVES)
            wide = pl.BlockSpec((seq, q_width), lambda b, h: (b + base, h))
            wide_in = pl.BlockSpec((seq, q_width), lambda b, h: (b + half_base, h))
            kv_spec = pl.BlockSpec((seq, KV_WIDTH), lambda b, h: (b, h))
            in_specs = [pl.BlockSpec(memory_space=pltpu.SMEM), pl.BlockSpec((seq, table_width), lambda b, h: (b + base, 0)), wide_in, wide_in] + [kv_spec] * 4
            aliases = {}
            if carried:
                in_specs += [pl.BlockSpec(memory_space=pl.ANY)] * 2
                aliases = {8: 0, 9: 1}
            full = jax.ShapeDtypeStruct((tokens, n_kv * q_width), jnp.bfloat16)
            part = jax.ShapeDtypeStruct((chunk_rows, kv_cols), jnp.float32)
            work = rows_b * n_kv * group * seq * 4 * seq
            return pl.pallas_call(
                attend_kernel, grid=(rows_b, n_kv), in_specs=in_specs, out_specs=[wide, wide] + [kv_spec] * 4,
                out_shape=[full, full] + [part] * 4, input_output_aliases=aliases,
                compiler_params=pltpu.CompilerParams(dimension_semantics=('arbitrary', 'arbitrary'), vmem_limit_bytes=48 * 1024 * 1024),
                cost_estimate=pl.CostEstimate(flops=work * HEAD_DIM * 12, bytes_accessed=chunk_rows * (n_kv * q_width * 10 + kv_cols * 24), transcendentals=work),
            )(flags, table, q_half[half], da_half[half], own[chunk], from_a[chunk], from_b[chunk], from_c[chunk], *carried)

        def add(left, right):
            return pl.pallas_call(
                add_kernel, grid=(rows_b,), in_specs=[row_spec(kv_cols)] * 2, out_specs=row_spec(kv_cols),
                out_shape=jax.ShapeDtypeStruct(left.shape, left.dtype), name='add_partial',
                cost_estimate=pl.CostEstimate(flops=chunk_rows * kv_cols * 300, bytes_accessed=chunk_rows * kv_cols * 12, transcendentals=0),
            )(left, right)

        carried = ()
        partials = []
        for c in range(CHUNKS):
            attn, dq_lin, d_own, d_a, d_b, d_c = attend(c, carried)
            carried = (attn, dq_lin)
            back_c = send(d_c, reverse(PAIRS_C))
            back_a = send(d_a, reverse(PAIRS_A))
            back_b = send(add(d_b, back_c), reverse(PAIRS_B))
            partials.append((d_own, back_a, back_b))

        out_proj = jnp.dot(attn, w_o, preferred_element_type=jnp.float32)
        out_tokens = (x_float + out_proj).astype(jnp.bfloat16)
        d_normed_q = jnp.einsum('tf,df->td', dq_lin, w_q, preferred_element_type=jnp.float32)
        d_normed_q = lax.optimization_barrier(d_normed_q)

        dkv_lin = None
        for c, (d_own, back_a, back_b) in enumerate(partials):
            base = c * rows_b
            in_specs = [row_spec(table_width, base)] + [row_spec(kv_cols)] * 3
            operands = [table, d_own, back_a, back_b]
            if dkv_lin is not None:
                in_specs.append(pl.BlockSpec(memory_space=pl.ANY))
                operands.append(dkv_lin)
            dkv_lin = pl.pallas_call(
                finish_kernel, grid=(rows_b,), in_specs=in_specs, out_specs=row_spec(kv_cols, base),
                out_shape=jax.ShapeDtypeStruct((tokens, kv_cols), jnp.bfloat16), input_output_aliases={4: 0} if c else {}, name='finish_kv',
                cost_estimate=pl.CostEstimate(flops=chunk_rows * kv_cols * 300, bytes_accessed=chunk_rows * kv_cols * 14, transcendentals=0),
            )(*operands)

        d_normed = (d_normed_q + jnp.einsum('tf,df->td', dkv_lin, w_kv, preferred_element_type=jnp.float32)).astype(jnp.bfloat16)
        d_gain = jnp.sum(d_normed * x_hat, axis=0)
        d_bias = jnp.sum(d_normed, axis=0, dtype=jnp.float32)
        d_hat = d_normed * (1.0 + ln_gain)
        d_x = inv_std * (d_hat - jnp.mean(d_hat, axis=-1, keepdims=True) - x_hat * jnp.mean(d_hat * x_hat, axis=-1, keepdims=True))
        dx_tokens = (dy_flat.astype(jnp.float32) + d_x).astype(jnp.bfloat16)
        return out_tokens.reshape(x_tokens.shape), dx_tokens.reshape(x_tokens.shape), d_gain, d_bias

    tok_spec = P('dp', 'sp', None)
    rep_vec = P(None)
    rep_mat = P(None, None)
    part_vec = P(('dp', 'sp'))
    return jax.shard_map(block_step, mesh=mesh,
                         in_specs=(tok_spec, tok_spec, P('dp', 'sp'), rep_vec, rep_vec, rep_mat, rep_mat, rep_mat, rep_mat),
                         out_specs=(tok_spec, tok_spec, part_vec, part_vec), check_vma=False)
```

time: 1970 us -> 1100 us (0.56)
  matrix products: 982 us -> 418 us
  local copies, waits for them, and re-layouts: 365 us -> 30.7 us
  Pallas kernels: 0 us -> 324 us
  waiting for transfers between devices: 436 us -> 165 us
    dot_general x13 -> x8, matrix products: 924 us -> 418 us  [the longest x2 86.2 us: block_step(): jnp.dot(normed[rows], w_q, preferred_element_type=jnp.float32)]
    all_to_all x8 -> x0, waiting for transfers between devices: 436 us -> none  [the longest x1 147 us: local_step(): lax.all_to_all(queries, 'sp', 2, 1, tiled=True)]
    pallas_call x0 -> x17, Pallas kernels: none -> 324 us  [the longest x4 238 us: attend(): pl.pallas_call(attend_kernel, grid=(rows_b, n_kv), in_specs=in_specs, out...]
    ppermute x0 -> x24, waiting for transfers between devices: none -> 165 us  [send(): return lax.ppermute(value, 'sp', pairs)]
    all_to_all x10 -> x0, local copies, waits for them, and re-layouts: 123 us -> none  [the longest x1 25.1 us: local_step(): lax.all_to_all(dq_heads.reshape(n_batch, seq_len, heads_loc, HEAD_DIM), '...]
    dot_general x3 -> x0, local copies, waits for them, and re-layouts: 78.3 us -> none  [the longest x1 41 us: local_step(): jnp.dot(normed_flat, w_q, preferred_element_type=jnp.float32)]
    all_to_all x8 -> x0, starting transfers between devices: 61 us -> none  [the longest x1 17 us: local_step(): k_heads = lax.all_to_all(key_rows, 'sp', 2, 1, tiled=True)]
    sub x1 -> x0, matrix products: 58.6 us -> none  [one_block(): attn_prob = jax.nn.softmax(scores, axis=-1).astype(jnp.bfloat16)]
  transfers between devices with their start and end apart: 8 -> 24, of which waited for: 5 -> 2; matrix products, arithmetic and copies ran while one was open for 38% -> 31% of each run, Pallas kernels for 0% -> 27%
where the time goes in v1:
time: 1100 us; the launch traced here: 1090 us
  matrix products  418 us (38%)
  Pallas kernels  324 us (29%)
  waiting for transfers between devices  165 us (15%)
  other arithmetic  99 us (9%)
  starting transfers between devices  51.6 us (5%)
  local copies, waits for them, and re-layouts  30.7 us (3%)
    pallas_call x4, Pallas kernels, attend(): pl.pallas_call(attend_kernel, grid=(rows_b, n_kv), in_specs=in_specs, out...  238 us
    ppermute x24, waiting for transfers between devices, send(): return lax.ppermute(value, 'sp', pairs)  165 us
    dot_general x2, matrix products, block_step(): jnp.dot(normed[rows], w_q, preferred_element_type=jnp.float32)  86.2 us
    dot_general x2, matrix products, block_step(): jnp.einsum('td,fd->tf', dy_flat[rows], w_o, preferred_element_type=jnp.fl...  85.3 us
    dot_general x1, matrix products, block_step(): out_proj = jnp.dot(attn, w_o, preferred_element_type=jnp.float32)  80.5 us
    dot_general x1, matrix products, block_step(): jnp.einsum('tf,df->td', dq_lin, w_q, preferred_element_type=jnp.float32)  79 us
    ppermute x24, starting transfers between devices, send(): return lax.ppermute(value, 'sp', pairs)  51.6 us
    dot_general x1, matrix products, block_step(): jnp.einsum('tf,df->td', dkv_lin, w_kv, preferred_element_type=jnp.float32)  43.8 us
  transfers between devices with their start and end apart: 24, of which 2 were waited for; matrix products, arithmetic and copies ran while one was open for 31% of the time, Pallas kernels for 27%

profile of v1, /device:TPU:0, one launch (start us, length us, event | category | flops | bytes accessed | tf_op | source)
XLA Modules:
  0.0 1090.1 jit_solution(1117823764241603728)
XLA Ops:
  1.5 8.7 convert_reduce_fusion.1
  11.3 5.5 fusion.10
  16.9 3.7 multiply_sine_fusion
  20.7 14.7 %join_kv.1 = bf16[4096,2048]{1,0:T(8,128)(2,1)} custom-call(bf16[4096,1024]{1,0:T(8,128)(2,1)} %wk_ref.1, bf16[4096,1024]{1,0:T(8,128)(2,1)} %wv_ref.1), custom_call_target="tpu_custom_call" | custom-call | flops 2516582400 | bytes 33554432 | tf_op jit(solution)/shard_map/join_kv/pallas_call | solution.py:163
  35.4 17.5 %fusion.15 = bf16[2048,4096]{1,0:T(8,128)(2,1)} fusion(bf16[16,128,4096]{2,1,0:T(8,128)(2,1)} %param.9, f32[4096]{0:T(1024)S(1)} %copy-done.14, f32[4096]{0:T(1024)S(1)} %broadcast_add_fusion, f32[2048]{0:T(1024)S(1)} %rsqrt_bitcast_fusion, f32[2048]{0:T(1024)S(1)} %get-tuple-element.62), kind=kLoop, calls=%fused_computation.22 | loop fusion | flops 50331648 | bytes 33603584 | tf_op jit(solution)/shard_map/convert_element_type | solution.py:160
  52.8 43.2 %fusion.24.lin_ref = f32[2048,2048]{1,0:T(8,128)} fusion(bf16[2048,4096]{1,0:T(8,128)(2,1)} %fusion.15, bf16[4096,2048]{1,0:T(8,128)(2,1)} %join_kv.1), kind=kOutput, calls=%fused_computation.44 | convolution fusion | flops 34359738368 | bytes 50331648 | tf_op jit(solution)/shard_map/dot_general | solution.py:168
  99.1 6.8 concatenate.15.table_ref
  105.9 5.1 pack_kv.4.rest_0_.own_ref
  111.0 6.4 collective-permute-start.10
  119.0 5.1 pack_kv.5.rest_0_.own_ref
  124.1 2.6 collective-permute-start.7
  126.7 2.7 collective-permute-start.6
  129.4 5.1 pack_kv.6.rest_0_.own_ref
  134.4 2.6 collective-permute-start.4
  137.1 43.2 %fusion.17.q_ref = f32[1024,4096]{1,0:T(8,128)} fusion(bf16[4096,4096]{1,0:T(8,128)(2,1)} %param.14, bf16[2048,4096]{1,0:T(8,128)(2,1)} %fusion.15), kind=kOutput, calls=%fused_computation.25 | convolution fusion | flops 34359738368 | bytes 58720256 | tf_op jit(solution)/shard_map/dot_general | solution.py:198
  180.2 43.0 %fusion.19.q_ref = f32[1024,4096]{1,0:T(8,128)} fusion(bf16[4096,4096]{1,0:T(8,128)(2,1)} %param.14, bf16[2048,4096]{1,0:T(8,128)(2,1)} %fusion.15), kind=kOutput, calls=%fused_computation.27 | convolution fusion | flops 34359738368 | bytes 58720256 | tf_op jit(solution)/shard_map/dot_general | solution.py:198
  223.3 5.1 pack_kv.7.own_ref
  228.4 12.3 %fusion.23 = (bf16[8,128,4096]{2,1,0:T(8,128)(2,1)}, bf16[8,128,4096]{2,1,0:T(8,128)(2,1)}) fusion(bf16[16,128,4096]{2,1,0:T(8,128)(2,1)} %param.10), kind=kLoop, calls=%fused_computation.43 | loop fusion | bytes 33554432 | tf_op jit(solution)/shard_map/slice | solution.py:199
  240.6 2.6 collective-permute-start.1
  244.6 2.0 collective-permute-start.11
  246.6 2.0 collective-permute-start.8
  248.6 42.7 %convolution_convert_fusion.do_ref = bf16[1024,4096]{1,0:T(8,128)(2,1)} fusion(bf16[1024,4096]{1,0:T(8,128)(2,1)} %bitcast.52, bf16[4096,4096]{1,0:T(8,128)(2,1)} %param.17), kind=kOutput, calls=%fused_computation.29 | convolution fusion | flops 34363932672 | bytes 50331648 | tf_op jit(solution)/shard_map/td,fd->tf/dot_general | solution.py:199
  296.1 59.3 %shard_map.120 = (bf16[2048,4096]{1,0:T(8,128)(2,1)}, bf16[2048,4096]{1,0:T(8,128)(2,1)}, f32[512,2048]{1,0:T(8,128)}, f32[512,2048]{1,0:T(8,128)}, f32[512,2048]{1,0:T(8,128)}, /*index=5*/f32[512,2048]{1,0:T(8,128)}) custom-call(s32[2]{0:T(128)S(1)} %pad_add_fusion.flags_ref, f32[2048,384]{1,0:T(8,128)} %concatenate.15.table_ref, ...), custom_call_target="tpu_custom_call" | custom-call | flops 12884901888 | bytes 46137344 | tf_op jit(solution)/shard_map/pallas_call | solution.py:216
  355.4 2.6 collective-permute-start
  359.9 2.1 collective-permute-start.2
  362.0 2.7 collective-permute-start.22
  364.7 59.5 %shard_map.121 = (bf16[2048,4096]{1,0:T(8,128)(2,1)}, bf16[2048,4096]{1,0:T(8,128)(2,1)}, f32[512,2048]{1,0:T(8,128)}, f32[512,2048]{1,0:T(8,128)}, f32[512,2048]{1,0:T(8,128)}, /*index=5*/f32[512,2048]{1,0:T(8,128)}) custom-call(s32[2]{0:T(128)S(1)} %pad_add_fusion.flags_ref, ...), custom_call_target="tpu_custom_call", output_to_operand_aliasing={{0}: (8, {}), {1}: (9, {})} | custom-call | flops 12884901888 | bytes 46137344 | tf_op jit(solution)/shard_map/pallas_call | solution.py:216
  425.6 2.6 collective-permute-start.19
  428.2 42.7 %convolution_convert_fusion.1.do_ref = bf16[1024,4096]{1,0:T(8,128)(2,1)} fusion(bf16[1024,4096]{1,0:T(8,128)(2,1)} %bitcast.51, bf16[4096,4096]{1,0:T(8,128)(2,1)} %param.17), kind=kOutput, calls=%fused_computation.30 | convolution fusion | flops 34363932672 | bytes 50331648 | tf_op jit(solution)/shard_map/td,fd->tf/dot_general | solution.py:199
  473.8 59.7 %shard_map.122 = (bf16[2048,4096]{1,0:T(8,128)(2,1)}, bf16[2048,4096]{1,0:T(8,128)(2,1)}, f32[512,2048]{1,0:T(8,128)}, f32[512,2048]{1,0:T(8,128)}, f32[512,2048]{1,0:T(8,128)}, /*index=5*/f32[512,2048]{1,0:T(8,128)}) custom-call(s32[2]{0:T(128)S(1)} %pad_add_fusion.flags_ref, ...), custom_call_target="tpu_custom_call", output_to_operand_aliasing={{0}: (8, {}), {1}: (9, {})} | custom-call | flops 12884901888 | bytes 46137344 | tf_op jit(solution)/shard_map/pallas_call | solution.py:216
  534.8 2.7 collective-permute-start.16
  537.5 59.5 %shard_map.123 = (bf16[2048,4096]{1,0:T(8,128)(2,1)}, bf16[2048,4096]{1,0:T(8,128)(2,1)}, f32[512,2048]{1,0:T(8,128)}, f32[512,2048]{1,0:T(8,128)}, f32[512,2048]{1,0:T(8,128)}, /*index=5*/f32[512,2048]{1,0:T(8,128)}) custom-call(s32[2]{0:T(128)S(1)} %pad_add_fusion.flags_ref, ...), custom_call_target="tpu_custom_call", output_to_operand_aliasing={{0}: (8, {}), {1}: (9, {})} | custom-call | flops 12884901888 | bytes 46137344 | tf_op jit(solution)/shard_map/pallas_call | solution.py:216
  597.1 2.6 collective-permute-start.13
  599.7 5.8 add_partial.7
  606.7 80.5 %fusion.16 = bf16[2048,4096]{1,0:T(8,128)(2,1)} fusion(bf16[16,128,4096]{2,1,0:T(8,128)(2,1)} %param.9, bf16[2048,4096]{1,0:T(8,128)(2,1)} %get-tuple-element.34, bf16[4096,4096]{1,0:T(8,128)(2,1)} %param.17), kind=kOutput, calls=%fused_computation.23 | convolution fusion | flops 68744642560 | bytes 83886080 | tf_op jit(solution)/shard_map/dot_general | solution.py:240
  687.2 5.8 add_partial.6
  694.3 5.8 add_partial.5
  701.4 5.8 add_partial.4
  711.0 79.0 %fusion.25 = f32[2048,4096]{1,0:T(8,128)} fusion(bf16[2048,4096]{1,0:T(8,128)(2,1)} %get-tuple-element.35, bf16[4096,4096]{1,0:T(8,128)(2,1)} %param.14), kind=kOutput, calls=%fused_computation.45 | convolution fusion | flops 68719476736 | bytes 83886080 | tf_op jit(solution)/shard_map/tf,df->td/dot_general | solution.py:242
  790.0 7.0 finish_kv.4.rest_0_
  797.0 7.0 finish_kv.5.rest_0_
  804.1 82.5 %collective-permute-done.17.b_ref = f32[512,2048]{1,0:T(8,128)} collective-permute-done((f32[512,2048]{1,0:T(8,128)}, f32[512,2048]{1,0:T(8,128)}, u32[]{:S(2)}, u32[]{:S(2)}) %collective-permute-start.17) | collective-permute-done | bytes 4194336 | tf_op jit(solution)/shard_map/ppermute | solution.py:185
  886.5 7.0 finish_kv.6.rest_0_
  893.6 82.9 %collective-permute-done.14.b_ref = f32[512,2048]{1,0:T(8,128)} collective-permute-done((f32[512,2048]{1,0:T(8,128)}, f32[512,2048]{1,0:T(8,128)}, u32[]{:S(2)}, u32[]{:S(2)}) %collective-permute-start.14) | collective-permute-done | bytes 4194336 | tf_op jit(solution)/shard_map/ppermute | solution.py:185
  976.4 7.0 finish_kv.7
  983.4 43.8 %fusion.26 = f32[2048,4096]{1,0:T(8,128)} fusion(bf16[2048,2048]{1,0:T(8,128)(2,1)} %finish_kv.7, bf16[4096,2048]{1,0:T(8,128)(2,1)} %join_kv.1), kind=kOutput, calls=%fused_computation.46 | convolution fusion | flops 34359738368 | bytes 58720256 | tf_op jit(solution)/shard_map/tf,df->td/dot_general | solution.py:259
  1027.2 34.0 %fusion.8 = (f32[4096]{0:T(1024)}, f32[2048]{0:T(1024)S(1)}, f32[2048]{0:T(1024)S(1)}, f32[4096]{0:T(1024)}, bf16[2048,4096]{1,0:T(8,128)(2,1)}) fusion(bf16[16,128,4096]{2,1,0:T(8,128)(2,1)} %param.9, f32[2048]{0:T(1024)S(1)} %copy-done.13, f32[2048]{0:T(1024)S(1)} %copy-done.11, f32[4096]{0:T(1024)S(1)} %copy-done.9, f32[2048,4096]{1,0:T(8,128)} %fusion.25, ...), kind=kLoop, calls=%fused_computation.11 | loop fusion | flops 109039616 | bytes 100745216 | tf_op jit(solution)/shard_map/reduce_sum | solution.py:260
  1061.3 28.6 %fusion.6 = bf16[2048,4096]{1,0:T(8,128)(2,1)} fusion(bf16[2048,4096]{1,0:T(8,128)(2,1)} %get-tuple-element.56, bf16[16,128,4096]{2,1,0:T(8,128)(2,1)} %param.9, bf16[16,128,4096]{2,1,0:T(8,128)(2,1)} %param.10, f32[2048]{0:T(1024)S(1)} %get-tuple-element.64, f32[2048]{0:T(1024)S(1)} %get-tuple-element.65, f32[4096]{0:T(1024)S(1)} %copy-done.9, ...), kind=kLoop, calls=%fused_computation.9 | loop fusion | flops 100663296 | bytes 67158016 | tf_op jit(solution)/shard_map/convert_element_type | solution.py:264
  (75 shorter events, 28.1 us)
Async XLA Ops:
  0.6 10.7 copy-start.7
  1.5 15.4 %copy-start.15 = (f32[4096]{0:T(1024)S(1)}, f32[4096]{0:T(1024)}, u32[]{:S(2)}) copy-start(f32[4096]{0:T(1024)} %param.12) | copy-start | bytes 49156
  10.2 25.1 %copy-start.10 = (f32[2048]{0:T(1024)}, f32[2048]{0:T(1024)S(1)}, u32[]{:S(2)}) copy-start(f32[2048]{0:T(1024)S(1)} %get-tuple-element.62) | copy-start | bytes 24580
  16.9 18.5 %copy-start.12 = (f32[2048]{0:T(1024)}, f32[2048]{0:T(1024)S(1)}, u32[]{:S(2)}) copy-start(f32[2048]{0:T(1024)S(1)} %rsqrt_bitcast_fusion) | copy-start | bytes 24580
  16.9 18.4 %copy-start.8 = (f32[4096]{0:T(1024)}, f32[4096]{0:T(1024)S(1)}, u32[]{:S(2)}) copy-start(f32[4096]{0:T(1024)S(1)} %broadcast_add_fusion) | copy-start | bytes 49156
  20.6 14.7 %copy-start.14 = (f32[4096]{0:T(1024)S(1)}, f32[4096]{0:T(1024)}, u32[]{:S(2)}) copy-start(f32[4096]{0:T(1024)} %param.13) | copy-start | bytes 49156
  111.0 129.6 %collective-permute-start.10 = (bf16[512,2048]{1,0:T(8,128)(2,1)}, bf16[512,2048]{1,0:T(8,128)(2,1)}, u32[]{:S(2)}, u32[]{:S(2)}) collective-permute-start(bf16[512,2048]{1,0:T(8,128)(2,1)} %pack_kv.4.rest_0_.own_ref), channel_id=1, source_target_pairs={{0,2},{1,3},{4,6},{5,7},{8,10},{9,11},{12,14},{13,15}} | collective-permute-start | bytes 6291464 | tf_op jit(solution)/shard_map/ppermute | solution.py:185
  117.4 125.8 %collective-permute-start.9 = (bf16[512,2048]{1,0:T(8,128)(2,1)}, bf16[512,2048]{1,0:T(8,128)(2,1)S(1)}, u32[]{:S(2)}, u32[]{:S(2)}) collective-permute-start(bf16[512,2048]{1,0:T(8,128)(2,1)} %pack_kv.4.rest_0_.own_ref), channel_id=1, source_target_pairs={{0,1},{2,3},{4,5},{6,7},{8,9},{10,11},{12,13},{14,15}} | collective-permute-start | bytes 6291464 | tf_op jit(solution)/shard_map/ppermute | solution.py:185
  124.1 122.5 %collective-permute-start.7 = (bf16[512,2048]{1,0:T(8,128)(2,1)}, bf16[512,2048]{1,0:T(8,128)(2,1)}, u32[]{:S(2)}, u32[]{:S(2)}) collective-permute-start(bf16[512,2048]{1,0:T(8,128)(2,1)} %pack_kv.5.rest_0_.own_ref), channel_id=1, source_target_pairs={{0,2},{1,3},{4,6},{5,7},{8,10},{9,11},{12,14},{13,15}} | collective-permute-start | bytes 6291464 | tf_op jit(solution)/shard_map/ppermute | solution.py:185
  126.7 228.7 %collective-permute-start.6 = (bf16[512,2048]{1,0:T(8,128)(2,1)}, bf16[512,2048]{1,0:T(8,128)(2,1)}, u32[]{:S(2)}, u32[]{:S(2)}) collective-permute-start(bf16[512,2048]{1,0:T(8,128)(2,1)} %pack_kv.5.rest_0_.own_ref), channel_id=1, source_target_pairs={{0,1},{2,3},{4,5},{6,7},{8,9},{10,11},{12,13},{14,15}} | collective-permute-start | bytes 6291464 | tf_op jit(solution)/shard_map/ppermute | solution.py:185
  134.4 223.5 %collective-permute-start.4 = (bf16[512,2048]{1,0:T(8,128)(2,1)}, bf16[512,2048]{1,0:T(8,128)(2,1)}, u32[]{:S(2)}, u32[]{:S(2)}) collective-permute-start(bf16[512,2048]{1,0:T(8,128)(2,1)} %pack_kv.6.rest_0_.own_ref), channel_id=1, source_target_pairs={{0,2},{1,3},{4,6},{5,7},{8,10},{9,11},{12,14},{13,15}} | collective-permute-start | bytes 6291464 | tf_op jit(solution)/shard_map/ppermute | solution.py:185
  240.6 119.3 %collective-permute-start.1 = (bf16[512,2048]{1,0:T(8,128)(2,1)}, bf16[512,2048]{1,0:T(8,128)(2,1)}, u32[]{:S(2)}, u32[]{:S(2)}) collective-permute-start(bf16[512,2048]{1,0:T(8,128)(2,1)} %pack_kv.7.own_ref), channel_id=1, source_target_pairs={{0,2},{1,3},{4,6},{5,7},{8,10},{9,11},{12,14},{13,15}} | collective-permute-start | bytes 6291464 | tf_op jit(solution)/shard_map/ppermute | solution.py:185
  243.2 1.4 copy-start.5
  244.6 46.8 %collective-permute-start.11 = (bf16[512,2048]{1,0:T(8,128)(2,1)}, bf16[512,2048]{1,0:T(8,128)(2,1)}, u32[]{:S(2)}, u32[]{:S(2)}) collective-permute-start(bf16[512,2048]{1,0:T(8,128)(2,1)} %collective-permute-done.10.b_ref), channel_id=1, source_target_pairs={{2,3},{3,2},{6,7},{7,6},{10,11},{11,10},{14,15},{15,14}} | collective-permute-start | bytes 6291464 | tf_op jit(solution)/shard_map/ppermute | solution.py:185
  246.6 115.4 %collective-permute-start.8 = (bf16[512,2048]{1,0:T(8,128)(2,1)}, bf16[512,2048]{1,0:T(8,128)(2,1)}, u32[]{:S(2)}, u32[]{:S(2)}) collective-permute-start(bf16[512,2048]{1,0:T(8,128)(2,1)} %collective-permute-done.7.b_ref), channel_id=1, source_target_pairs={{2,3},{3,2},{6,7},{7,6},{10,11},{11,10},{14,15},{15,14}} | collective-permute-start | bytes 6291464 | tf_op jit(solution)/shard_map/ppermute | solution.py:185
  248.6 42.8 %copy-start = (bf16[512,2048]{1,0:T(8,128)(2,1)S(1)}, bf16[512,2048]{1,0:T(8,128)(2,1)}, u32[]{:S(2)}) copy-start(bf16[512,2048]{1,0:T(8,128)(2,1)} %pack_kv.6.rest_0_.own_ref) | copy-start | bytes 6291460
  291.4 73.3 %copy-start.1 = (bf16[512,2048]{1,0:T(8,128)(2,1)S(1)}, bf16[512,2048]{1,0:T(8,128)(2,1)}, u32[]{:S(2)}) copy-start(bf16[512,2048]{1,0:T(8,128)(2,1)} %pack_kv.5.rest_0_.own_ref) | copy-start | bytes 6291460
  291.4 132.8 %collective-permute-start.3 = (bf16[512,2048]{1,0:T(8,128)(2,1)S(1)}, bf16[512,2048]{1,0:T(8,128)(2,1)S(1)}, u32[]{:S(2)}, u32[]{:S(2)}) collective-permute-start(bf16[512,2048]{1,0:T(8,128)(2,1)S(1)} %copy-done), channel_id=1, source_target_pairs={{0,1},{2,3},{4,5},{6,7},{8,9},{10,11},{12,13},{14,15}} | collective-permute-start | bytes 6291464 | tf_op jit(solution)/shard_map/ppermute | solution.py:185
  292.9 1.6 copy-start.2
  294.5 1.6 copy-start.6
  355.4 178.1 %collective-permute-start = (bf16[512,2048]{1,0:T(8,128)(2,1)}, bf16[512,2048]{1,0:T(8,128)(2,1)}, u32[]{:S(2)}, u32[]{:S(2)}) collective-permute-start(bf16[512,2048]{1,0:T(8,128)(2,1)} %pack_kv.7.own_ref), channel_id=1, source_target_pairs={{0,1},{2,3},{4,5},{6,7},{8,9},{10,11},{12,13},{14,15}} | collective-permute-start | bytes 6291464 | tf_op jit(solution)/shard_map/ppermute | solution.py:185
  358.0 112.9 %collective-permute-start.5 = (bf16[512,2048]{1,0:T(8,128)(2,1)}, bf16[512,2048]{1,0:T(8,128)(2,1)}, u32[]{:S(2)}, u32[]{:S(2)}) collective-permute-start(bf16[512,2048]{1,0:T(8,128)(2,1)} %collective-permute-done.4.b_ref), channel_id=1, source_target_pairs={{2,3},{3,2},{6,7},{7,6},{10,11},{11,10},{14,15},{15,14}} | collective-permute-start | bytes 6291464 | tf_op jit(solution)/shard_map/ppermute | solution.py:185
  359.9 174.9 %collective-permute-start.2 = (bf16[512,2048]{1,0:T(8,128)(2,1)}, bf16[512,2048]{1,0:T(8,128)(2,1)}, u32[]{:S(2)}, u32[]{:S(2)}) collective-permute-start(bf16[512,2048]{1,0:T(8,128)(2,1)} %collective-permute-done.1.b_ref), channel_id=1, source_target_pairs={{2,3},{3,2},{6,7},{7,6},{10,11},{11,10},{14,15},{15,14}} | collective-permute-start | bytes 6291464 | tf_op jit(solution)/shard_map/ppermute | solution.py:185
  362.0 235.0 %collective-permute-start.22 = (f32[512,2048]{1,0:T(8,128)}, f32[512,2048]{1,0:T(8,128)}, u32[]{:S(2)}, u32[]{:S(2)}) collective-permute-start(f32[512,2048]{1,0:T(8,128)} %get-tuple-element.51), channel_id=1, source_target_pairs={{3,2},{2,3},{7,6},{6,7},{11,10},{10,11},{15,14},{14,15}} | collective-permute-start | bytes 12582920 | tf_op jit(solution)/shard_map/ppermute | solution.py:185
  424.2 1.4 copy-start.3
  425.6 179.9 %collective-permute-start.19 = (f32[512,2048]{1,0:T(8,128)}, f32[512,2048]{1,0:T(8,128)}, u32[]{:S(2)}, u32[]{:S(2)}) collective-permute-start(f32[512,2048]{1,0:T(8,128)} %get-tuple-element.47), channel_id=1, source_target_pairs={{3,2},{2,3},{7,6},{6,7},{11,10},{10,11},{15,14},{14,15}} | collective-permute-start | bytes 12582920 | tf_op jit(solution)/shard_map/ppermute | solution.py:185
  470.9 236.2 %collective-permute-start.21 = (f32[512,2048]{1,0:T(8,128)}, f32[512,2048]{1,0:T(8,128)}, u32[]{:S(2)}, u32[]{:S(2)}) collective-permute-start(f32[512,2048]{1,0:T(8,128)} %get-tuple-element.49), channel_id=1, source_target_pairs={{1,0},{3,2},{5,4},{7,6},{9,8},{11,10},{13,12},{15,14}} | collective-permute-start | bytes 12582920 | tf_op jit(solution)/shard_map/ppermute | solution.py:185
  472.2 1.6 copy-start.4
  533.5 174.9 %collective-permute-start.18 = (f32[512,2048]{1,0:T(8,128)}, f32[512,2048]{1,0:T(8,128)}, u32[]{:S(2)}, u32[]{:S(2)}) collective-permute-start(f32[512,2048]{1,0:T(8,128)} %get-tuple-element.45), channel_id=1, source_target_pairs={{1,0},{3,2},{5,4},{7,6},{9,8},{11,10},{13,12},{15,14}} | collective-permute-start | bytes 12582920 | tf_op jit(solution)/shard_map/ppermute | solution.py:185
  534.8 158.2 %collective-permute-start.16 = (f32[512,2048]{1,0:T(8,128)}, f32[512,2048]{1,0:T(8,128)}, u32[]{:S(2)}, u32[]{:S(2)}) collective-permute-start(f32[512,2048]{1,0:T(8,128)} %get-tuple-element.43), channel_id=1, source_target_pairs={{3,2},{2,3},{7,6},{6,7},{11,10},{10,11},{15,14},{14,15}} | collective-permute-start | bytes 12582920 | tf_op jit(solution)/shard_map/ppermute | solution.py:185
  597.1 103.0 %collective-permute-start.13 = (f32[512,2048]{1,0:T(8,128)}, f32[512,2048]{1,0:T(8,128)}, u32[]{:S(2)}, u32[]{:S(2)}) collective-permute-start(f32[512,2048]{1,0:T(8,128)} %get-tuple-element.39), channel_id=1, source_target_pairs={{3,2},{2,3},{7,6},{6,7},{11,10},{10,11},{15,14},{14,15}} | collective-permute-start | bytes 12582920 | tf_op jit(solution)/shard_map/ppermute | solution.py:185
  605.5 104.3 %collective-permute-start.23 = (f32[512,2048]{1,0:T(8,128)}, f32[512,2048]{1,0:T(8,128)}, u32[]{:S(2)}, u32[]{:S(2)}) collective-permute-start(f32[512,2048]{1,0:T(8,128)} %add_partial.7), channel_id=1, source_target_pairs={{2,0},{3,1},{6,4},{7,5},{10,8},{11,9},{14,12},{15,13}} | collective-permute-start | bytes 12582920 | tf_op jit(solution)/shard_map/ppermute | solution.py:185
  693.0 111.1 %collective-permute-start.15 = (f32[512,2048]{1,0:T(8,128)}, f32[512,2048]{1,0:T(8,128)}, u32[]{:S(2)}, u32[]{:S(2)}) collective-permute-start(f32[512,2048]{1,0:T(8,128)} %get-tuple-element.41), channel_id=1, source_target_pairs={{1,0},{3,2},{5,4},{7,6},{9,8},{11,10},{13,12},{15,14}} | collective-permute-start | bytes 12582920 | tf_op jit(solution)/shard_map/ppermute | solution.py:185
  700.1 193.5 %collective-permute-start.12 = (f32[512,2048]{1,0:T(8,128)}, f32[512,2048]{1,0:T(8,128)}, u32[]{:S(2)}, u32[]{:S(2)}) collective-permute-start(f32[512,2048]{1,0:T(8,128)} %get-tuple-element.37), channel_id=1, source_target_pairs={{1,0},{3,2},{5,4},{7,6},{9,8},{11,10},{13,12},{15,14}} | collective-permute-start | bytes 12582920 | tf_op jit(solution)/shard_map/ppermute | solution.py:185
  707.1 89.9 %collective-permute-start.20 = (f32[512,2048]{1,0:T(8,128)}, f32[512,2048]{1,0:T(8,128)}, u32[]{:S(2)}, u32[]{:S(2)}) collective-permute-start(f32[512,2048]{1,0:T(8,128)} %add_partial.6), channel_id=1, source_target_pairs={{2,0},{3,1},{6,4},{7,5},{10,8},{11,9},{14,12},{15,13}} | collective-permute-start | bytes 12582920 | tf_op jit(solution)/shard_map/ppermute | solution.py:185
  708.4 178.1 %collective-permute-start.17 = (f32[512,2048]{1,0:T(8,128)}, f32[512,2048]{1,0:T(8,128)}, u32[]{:S(2)}, u32[]{:S(2)}) collective-permute-start(f32[512,2048]{1,0:T(8,128)} %add_partial.5), channel_id=1, source_target_pairs={{2,0},{3,1},{6,4},{7,5},{10,8},{11,9},{14,12},{15,13}} | collective-permute-start | bytes 12582920 | tf_op jit(solution)/shard_map/ppermute | solution.py:185
  709.7 266.7 %collective-permute-start.14 = (f32[512,2048]{1,0:T(8,128)}, f32[512,2048]{1,0:T(8,128)}, u32[]{:S(2)}, u32[]{:S(2)}) collective-permute-start(f32[512,2048]{1,0:T(8,128)} %add_partial.4), channel_id=1, source_target_pairs={{2,0},{3,1},{6,4},{7,5},{10,8},{11,9},{14,12},{15,13}} | collective-permute-start | bytes 12582920 | tf_op jit(solution)/shard_map/ppermute | solution.py:185
  983.4 43.8 %copy-start.9 = (f32[4096]{0:T(1024)S(1)}, f32[4096]{0:T(1024)}, u32[]{:S(2)}) copy-start(f32[4096]{0:T(1024)} %copy-done.8) | copy-start | bytes 49156
  983.4 43.8 %copy-start.11 = (f32[2048]{0:T(1024)S(1)}, f32[2048]{0:T(1024)}, u32[]{:S(2)}) copy-start(f32[2048]{0:T(1024)} %copy-done.10) | copy-start | bytes 24580
  983.4 43.8 %copy-start.13 = (f32[2048]{0:T(1024)S(1)}, f32[2048]{0:T(1024)}, u32[]{:S(2)}) copy-start(f32[2048]{0:T(1024)} %copy-done.12) | copy-start | bytes 24580
